TPU v7x, 32 devices: a whole 2x2x4 slice. The times are simulated.
32 devices in a mesh: dp: 2 (over x), expert: 8 (over z, y), tensor: 2 (over core).
Axes of the slice: x: 2, y: 2, z: 4, core: 2. Of those that a mesh axis runs over, the one named last changes fastest.
Arguments:
- tokens: bfloat16 [2048, 2048], P(('dp', 'expert')), may hold values from -6 to 6
- norm_gain: float32 [2048], replicated, may hold values from 0.1 to 1.9
- router: bfloat16 [2048, 8], replicated, may hold values from -0.125 to 0.125
- expert_ids: int32 [2048, 4], P(('dp', 'expert')), may hold values from 0 to 7, all different within a row; in each aligned block of 128 rows (0 to 127, 128 to 255, ...) at most 80 rows name the same one
- modality: int32 [2048], P(('dp', 'expert')), may hold values from 0 to 1, as said below
- expert_gate: bfloat16 [8, 2048, 1408], P('expert', None, 'tensor'), may hold values from -0.125 to 0.125
- expert_up: bfloat16 [8, 2048, 1408], P('expert', None, 'tensor'), may hold values from -0.125 to 0.125
- expert_down: bfloat16 [8, 1408, 2048], P('expert', 'tensor'), may hold values from -0.15625 to 0.15625
- shared_gate: bfloat16 [2, 2048, 704], P(None, None, ('dp', 'tensor')), may hold values from -0.125 to 0.125
- shared_up: bfloat16 [2, 2048, 704], P(None, None, ('dp', 'tensor')), may hold values from -0.125 to 0.125
- shared_down: bfloat16 [2, 704, 2048], P(None, ('dp', 'tensor')), may hold values from -0.21875 to 0.21875
Outputs:
- mixed: bfloat16 [2048, 2048], P(('dp', 'expert'), 'tensor')
Inputs may be any that keep to these rules, and one draw needn't show every extreme that they name: `expert_ids`: each token names 4 different experts; among the 128 tokens of one device (aligned blocks of rows) no expert is named by more than 80 tokens, and some expert reaches 80. `modality`: within each aligned block of 128 tokens the image patches form one run (taken cyclically) that covers from an eighth to seven eighths of the block.
All inputs are finite; a program needn't handle non-finite values.
Results may differ from a plain program's by a relative error of at most 0.0073.
Values may be sent and summed in bfloat16 or wider, within the bound.
A program may use at most 128 MiB of HBM per device.

v0:
```python
import jax
import jax.numpy as jnp
from jax import lax
from jax.sharding import PartitionSpec as P

epsilon = 1e-06


def rms_normed(tokens, norm_gain):
    values = tokens.astype(jnp.float32)
    inv_scale = lax.rsqrt(jnp.mean(values * values, axis=-1, keepdims=True) + epsilon)
    return (values * inv_scale * norm_gain).astype(jnp.bfloat16)


def route_weights(normed, router, expert_ids):
    logits = jnp.dot(normed, router, preferred_element_type=jnp.float32)
    chosen = jnp.take_along_axis(logits, expert_ids, axis=1)
    scores = jax.nn.sigmoid(chosen)
    return scores / jnp.sum(scores, axis=1, keepdims=True)


def capacity_slots(expert_ids, expert_count, block_rows):
    row_count, top_count = expert_ids.shape
    onehot = (
        expert_ids[:, :, None] == jnp.arange(expert_count, dtype=jnp.int32)[None, None, :]
    ).astype(jnp.int32)
    grouped = onehot.reshape(row_count // block_rows, block_rows * top_count, expert_count)
    running = (jnp.cumsum(grouped, axis=1, dtype=jnp.int32) - 1).reshape(
        row_count, top_count, expert_count
    )
    return jnp.sum(running * onehot, axis=-1, dtype=jnp.int32)


def per_device(
    tokens,
    norm_gain,
    router,
    expert_ids,
    modality,
    expert_gate,
    expert_up,
    expert_down,
    shared_gate,
    shared_up,
    shared_down,
):
    normed = rms_normed(tokens, norm_gain)
    weights = route_weights(normed, router, expert_ids)
    tok_rows, model_width = normed.shape
    top_count = expert_ids.shape[1]
    groups = lax.axis_size("expert")
    pair_count = lax.axis_size("tensor")
    dp_count = lax.axis_size("dp")
    half_width = model_width // pair_count
    expert_count = groups * expert_gate.shape[0]
    capacity = pair_count * (
        (5 * tok_rows * top_count + 4 * expert_count * pair_count - 1)
        // (4 * expert_count * pair_count)
    )
    slot_rank = capacity_slots(expert_ids, expert_count, tok_rows)
    target = expert_ids * capacity + slot_rank
    positions = jnp.arange(expert_count * capacity, dtype=jnp.int32)
    placing = jnp.any(positions[:, None, None] == target[None, :, :], axis=2).astype(jnp.bfloat16)
    outgoing = jnp.dot(placing, normed, preferred_element_type=jnp.float32).astype(jnp.bfloat16)
    outgoing = outgoing.reshape(groups, capacity, model_width)
    received = lax.all_to_all(outgoing, "expert", split_axis=0, concat_axis=0, tiled=True)
    flat_rows = received.reshape(-1, model_width)
    gate_value = jnp.dot(flat_rows, expert_gate[0], preferred_element_type=jnp.float32)
    up_value = jnp.dot(flat_rows, expert_up[0], preferred_element_type=jnp.float32)
    hidden = (jax.nn.silu(gate_value) * up_value).astype(jnp.bfloat16)
    result = jnp.dot(hidden, expert_down[0], preferred_element_type=jnp.float32)
    partials = result.reshape(received.shape[0], received.shape[1], model_width)
    reduced = lax.psum_scatter(partials, "tensor", scatter_dimension=2, tiled=True)
    returned = lax.all_to_all(reduced, "expert", split_axis=0, concat_axis=0, tiled=True)
    picked = returned.reshape(-1, returned.shape[2])[target]
    routed = jnp.sum(weights[:, :, None] * picked, axis=1)
    everyone, kind_flags = (
        lax.all_gather(normed, "dp", axis=0, tiled=True),
        lax.all_gather(modality, "dp", axis=0, tiled=True),
    )
    image_flag = kind_flags.astype(jnp.float32)[:, None]

    def shared_hidden(modal_index, keep):
        gate_value = jnp.dot(everyone, shared_gate[modal_index], preferred_element_type=jnp.float32)
        up_value = jnp.dot(everyone, shared_up[modal_index], preferred_element_type=jnp.float32)
        return (jax.nn.silu(gate_value) * up_value * keep).astype(jnp.bfloat16)

    joined = jnp.concatenate(
        [shared_hidden(0, image_flag), shared_hidden(1, 1.0 - image_flag)], axis=1
    )
    down_blocks = shared_down.reshape(-1, pair_count, half_width)
    split_rows = joined.reshape(dp_count, tok_rows, joined.shape[1])
    shared_term = jnp.einsum(
        "pks,std->ptkd", split_rows, down_blocks, preferred_element_type=jnp.float32
    )
    shared_sum = lax.psum_scatter(
        shared_term.reshape(-1, half_width), ("dp", "tensor"), scatter_dimension=0, tiled=True
    )
    total = shared_sum + routed
    return total.astype(jnp.bfloat16)


def solution(mesh):
    in_specs = (
        P(("dp", "expert"), None),
        P(),
        P(),
        P(("dp", "expert"), None),
        P(("dp", "expert")),
        P("expert", None, "tensor"),
        P("expert", None, "tensor"),
        P("expert", "tensor", None),
        P(None, None, ("dp", "tensor")),
        P(None, None, ("dp", "tensor")),
        P(None, ("dp", "tensor"), None),
    )
    out_specs = P(("dp", "expert"), "tensor")
    return jax.shard_map(
        per_device, mesh=mesh, in_specs=in_specs, out_specs=out_specs, check_vma=False
    )
```

profile of v0, /device:TPU:0, one launch (start us, length us, event | category | flops | bytes accessed | tf_op | source)
XLA Modules:
  0.0 199.3 jit_solution(18202294359154056301)
XLA Ops:
  7.4 0.9 copy.56
  8.4 1.1 reduce-window.6
  11.0 1.2 fusion.16
  12.2 1.2 fusion.18
  13.5 2.4 %convolution_convert_fusion = bf16[640,2048]{1,0:T(8,128)(2,1)} fusion(pred[640,128]{1,0:T(8,128)(4,1)S(1)} %fusion.11, bf16[128,2048]{1,0:T(8,128)(2,1)S(1)} %fusion.18), kind=kOutput, calls=%fused_computation.2 | convolution fusion | flops 336855040 | bytes 3227648 | tf_op jit(solution)/shard_map/dot_general | solution.py:64
  15.8 7.3 %all-to-all-start = ((bf16[8,80,2048]{2,1,0:T(8,128)(2,1)}), bf16[8,80,2048]{2,1,0:T(8,128)(2,1)}, u32[]{:S(2)}, u32[]{:S(2)}) async-start(bf16[8,80,2048]{2,1,0:T(8,128)(2,1)} %bitcast.73), calls=%async_computation.1 | async-start | bytes 5242880 | tf_op jit(solution)/shard_map/all_to_all | solution.py:66
  23.9 58.8 %all-to-all-done = bf16[8,80,2048]{2,1,0:T(8,128)(2,1)} async-done(((bf16[8,80,2048]{2,1,0:T(8,128)(2,1)}), bf16[8,80,2048]{2,1,0:T(8,128)(2,1)}, u32[]{:S(2)}, u32[]{:S(2)}) %all-to-all-start) | async-done | bytes 2621472 | tf_op jit(solution)/shard_map/all_to_all | solution.py:66
  82.7 5.2 %fusion.4 = f32[640,704]{0,1:T(8,128)S(1)} fusion(bf16[640,2048]{1,0:T(8,128)(2,1)} %bitcast.18, bf16[1,2048,704]{1,2,0:T(8,128)(2,1)} %param.16), kind=kOutput, calls=%fused_computation.7 | convolution fusion | flops 1845493760 | bytes 7307264 | tf_op jit(solution)/shard_map/dot_general | solution.py:68
  87.9 5.2 %multiply_convert_fusion = bf16[640,704]{0,1:T(8,128)(2,1)} fusion(f32[640,704]{0,1:T(8,128)S(1)} %fusion.4, bf16[640,2048]{1,0:T(8,128)(2,1)} %bitcast.18, bf16[1,2048,704]{1,2,0:T(8,128)(2,1)S(1)} %copy-done.5), kind=kOutput, calls=%fused_computation.10 | convolution fusion | flops 1848197120 | bytes 8208384 | tf_op jit(solution)/shard_map/dot_general | solution.py:69
  93.1 2.3 %copy.58 = bf16[640,704]{1,0:T(8,128)(2,1)} copy(bf16[640,704]{0,1:T(8,128)(2,1)} %multiply_convert_fusion) | data formatting | bytes 1802240 | tf_op jit(solution)/shard_map/convert_element_type | solution.py:70
  95.4 5.7 %fusion = f32[8,80,2048]{2,1,0:T(8,128)} fusion(bf16[8,80,704]{2,1,0:T(8,128)(2,1)} %bitcast.75, bf16[1,704,2048]{2,1,0:T(8,128)(2,1)S(1)} %copy-done), kind=kOutput, calls=%fused_computation.3 | convolution fusion | flops 1845493760 | bytes 9027584 | tf_op jit(solution)/shard_map/dot_general | solution.py:71
  101.8 4.2 %all-gather = s32[2,1,128]{2,1,0:T(1,128)S(1)} all-gather(s32[1,1,128]{2,1,0:T(1,128)S(1)} %bitcast.80), channel_id=1, replica_groups=mesh['dp'=2,'expert'=8,'tensor'=2] {'dp'}, dimensions={0}, use_global_device_ids=true | all-gather | bytes 1536 | tf_op jit(solution)/shard_map/all_gather | solution.py:79
  106.0 4.9 %reshape.152 = bf16[352,2,1024]{2,1,0:T(2,128)(2,1)} reshape(bf16[2,176,2048]{2,1,0:T(8,128)(2,1)} %param.21) | data formatting | bytes 2883584 | tf_op jit(solution)/shard_map/reshape | solution.py:91
  111.0 2.2 %fusion.20 = f32[256,176]{0,1:T(8,128)S(1)} fusion(bf16[256,2048]{1,0:T(8,128)(2,1)} %all-gather.3.cloned.1.call-done, bf16[2,2048,176]{1,2,0:T(8,128)(2,1)} %param.19), kind=kOutput, calls=%fused_computation.28 | convolution fusion | flops 184549376 | bytes 1949696 | tf_op jit(solution)/shard_map/dot_general | solution.py:84
  113.2 1.9 fusion.23
  115.7 4.4 %all-to-all-start.1 = ((f32[8,80,1024]{2,1,0:T(8,128)}), f32[8,80,1024]{2,1,0:T(8,128)}, u32[]{:S(2)}, u32[]{:S(2)}) async-start(f32[8,80,1024]{2,1,0:T(8,128)} %reduce-scatter.5.cloned.1.call-done), calls=%async_computation.3 | async-start | bytes 5242880 | tf_op jit(solution)/shard_map/all_to_all | solution.py:74
  120.3 1.9 fusion.15
  122.3 3.4 %fusion.8 = f32[2,128,2,1024]{3,1,2,0:T(8,128)} fusion(bf16[352,2,1024]{2,1,0:T(2,128)(2,1)} %reshape.152, bf16[2,128,352,1]{1,0,2,3:T(2,128)(2,1)S(1)} %bitcast.76), kind=kOutput, calls=%fused_computation.11 | convolution fusion | flops 369098752 | bytes 3719168 | tf_op jit(solution)/shard_map/pks,std->ptkd/dot_general | solution.py:93
  127.0 2.6 %gather_fusion.1 = f32[512]{0:T(512)S(1)} fusion(f32[128,8]{0,1:T(8,128)S(1)} %fusion.32, s32[512]{0:T(512)S(1)} %reshape.172), kind=kCustom, calls=%fused_computation.1 | custom fusion | bytes 8192 | tf_op jit(solution)/shard_map/jit(take_along_axis)/gather | solution.py:17
  130.0 48.9 %all-to-all-done.1 = f32[8,80,1024]{2,1,0:T(8,128)} async-done(((f32[8,80,1024]{2,1,0:T(8,128)}), f32[8,80,1024]{2,1,0:T(8,128)}, u32[]{:S(2)}, u32[]{:S(2)}) %all-to-all-start.1) | async-done | bytes 2621472 | tf_op jit(solution)/shard_map/all_to_all | solution.py:74
  178.8 5.4 %gather_fusion = f32[512,1024]{1,0:T(8,128)} fusion(f32[640,1024]{1,0:T(8,128)} %bitcast.24, s32[1024]{0:T(1024)S(1)} %pad_clamp_fusion), kind=kCustom, calls=%fused_computation | custom fusion | bytes 4196352 | tf_op jit(solution)/shard_map/gather | solution.py:75
  184.2 2.9 %reshape.165 = f32[128,4,1024]{2,1,0:T(4,128)} reshape(f32[512,1024]{1,0:T(8,128)} %gather_fusion) | data formatting | bytes 4194304 | tf_op jit(solution)/shard_map/gather | solution.py:75
  187.1 3.0 %multiply_reduce_fusion = f32[128,1024]{1,0:T(8,128)S(1)} fusion(f32[128,4,1024]{2,1,0:T(4,128)} %reshape.165, f32[128,4]{1,0:T(8,128)S(1)} %copy.55), kind=kLoop, calls=%fused_computation.9 | loop fusion | flops 917504 | bytes 2623488 | tf_op jit(solution)/shard_map/reduce_sum | solution.py:76
  190.1 1.8 add_convert_fusion
  (55 shorter events, 5.4 us)
Async XLA Ops:
  7.4 88.0 %copy-start = (bf16[1,704,2048]{2,1,0:T(8,128)(2,1)S(1)}, bf16[1,704,2048]{2,1,0:T(8,128)(2,1)}, u32[]{:S(2)}) copy-start(bf16[1,704,2048]{2,1,0:T(8,128)(2,1)} %param.18) | copy-start | bytes 8650756
  13.5 2.4 %copy-start.1 = (bf16[128,2048]{1,0:T(8,128)(2,1)}, bf16[128,2048]{1,0:T(8,128)(2,1)S(1)}, u32[]{:S(2)}) copy-start(bf16[128,2048]{1,0:T(8,128)(2,1)S(1)} %fusion.18) | copy-start | bytes 1572868
  15.8 66.9 %all-to-all-start = ((bf16[8,80,2048]{2,1,0:T(8,128)(2,1)}), bf16[8,80,2048]{2,1,0:T(8,128)(2,1)}, u32[]{:S(2)}, u32[]{:S(2)}) async-start(bf16[8,80,2048]{2,1,0:T(8,128)(2,1)} %bitcast.73), calls=%async_computation.1 | async-start | bytes 5242880 | tf_op jit(solution)/shard_map/all_to_all | solution.py:66
  23.1 87.8 %all-gather.3.cloned.1.call-start = ((), (), s32[]{:S(2)}) async-start(), calls=%async_computation.4 | async-start | bytes 1572864 | tf_op jit(solution)/shard_map/all_gather | solution.py:78
  23.9 91.8 %reduce-scatter.5.cloned.1.call-start = ((), (), s32[]{:S(2)}) async-start(), calls=%async_computation.6 | async-start | bytes 7864320 | tf_op jit(solution)/shard_map/reduce_scatter | solution.py:73
  82.7 5.2 %copy-start.5 = (bf16[1,2048,704]{1,2,0:T(8,128)(2,1)S(1)}, bf16[1,2048,704]{1,2,0:T(8,128)(2,1)}, u32[]{:S(2)}) copy-start(bf16[1,2048,704]{1,2,0:T(8,128)(2,1)} %param.17) | copy-start | bytes 8650756
  101.1 0.7 copy-start.8
  110.9 4.2 %copy-start.6 = (bf16[2,2048,176]{1,2,0:T(8,128)(2,1)S(1)}, bf16[2,2048,176]{1,2,0:T(8,128)(2,1)}, u32[]{:S(2)}) copy-start(bf16[2,2048,176]{1,2,0:T(8,128)(2,1)} %param.20) | copy-start | bytes 4325380
  110.9 4.2 %copy-start.7 = (bf16[256,2048]{1,0:T(8,128)(2,1)S(1)}, bf16[256,2048]{1,0:T(8,128)(2,1)}, u32[]{:S(2)}) copy-start(bf16[256,2048]{1,0:T(8,128)(2,1)} %all-gather.3.cloned.1.call-done) | copy-start | bytes 3145732
  115.7 63.2 %all-to-all-start.1 = ((f32[8,80,1024]{2,1,0:T(8,128)}), f32[8,80,1024]{2,1,0:T(8,128)}, u32[]{:S(2)}, u32[]{:S(2)}) async-start(f32[8,80,1024]{2,1,0:T(8,128)} %reduce-scatter.5.cloned.1.call-done), calls=%async_computation.3 | async-start | bytes 5242880 | tf_op jit(solution)/shard_map/all_to_all | solution.py:74
  120.1 70.0 %reduce-scatter.3.cloned.1.call-start = ((), (), s32[]{:S(2)}) async-start(), calls=%async_computation.5 | async-start | bytes 2621440 | tf_op jit(solution)/shard_map/reduce_scatter | solution.py:96
  122.3 3.7 %copy-start.3 = (s32[128,4]{0,1:T(4,128)S(1)}, s32[128,4]{0,1:T(4,128)}, u32[]{:S(2)}) copy-start(s32[128,4]{0,1:T(4,128)} %param.14) | copy-start | bytes 6148
  125.8 1.0 copy-start.2
  125.8 1.0 copy-start.4
Sparse Core Ops, SparseCore 0:
  25.5 22.6 all-gather.2
  125.9 32.3 reduce-scatter.2
Sparse Core Ops, SparseCore 1:
  101.2 11.8 reduce-scatter.4
where the time goes:
time: 200 us; the launch traced here: 199 us
  waiting for transfers between devices  108 us (54%)
  matrix products  28.7 us (14%)
  local copies, waits for them, and re-layouts  21.4 us (11%)
  between operations  15.1 us (8%)
  starting transfers between devices  12 us (6%)
  other arithmetic  9.49 us (5%)
  blocking collectives  4.22 us (2%)
    all_to_all x1, waiting for transfers between devices, per_device(): lax.all_to_all(outgoing, 'expert', split_axis=0, concat_axis=0, tiled=True)  58.8 us
    all_to_all x1, waiting for transfers between devices, per_device(): lax.all_to_all(reduced, 'expert', split_axis=0, concat_axis=0, tiled=True)  48.9 us
    gather x2, local copies, waits for them, and re-layouts, per_device(): picked = returned.reshape(-1, returned.shape[2])[target]  8.24 us
    all_to_all x1, starting transfers between devices, per_device(): lax.all_to_all(outgoing, 'expert', split_axis=0, concat_axis=0, tiled=True)  7.31 us
    dot_general x1, matrix products, per_device(): result = jnp.dot(hidden, expert_down[0], preferred_element_type=jnp.float32)  5.71 us
    dot_general x1, matrix products, per_device(): jnp.dot(flat_rows, expert_up[0], preferred_element_type=jnp.float32)  5.19 us
    dot_general x1, matrix products, per_device(): jnp.dot(flat_rows, expert_gate[0], preferred_element_type=jnp.float32)  5.19 us
    reshape x1, local copies, waits for them, and re-layouts, per_device(): down_blocks = shared_down.reshape(-1, pair_count, half_width)  4.94 us
  transfers between devices with their start and end apart: 5, of which 2 were waited for; matrix products, arithmetic and copies ran while one was open for 24% of the time, Pallas kernels for 0%

commit v1 on v0

--- a/solution.py
+++ b/solution.py
@@ -1,7 +1,10 @@
 import jax
 import jax.numpy as jnp
 from jax import lax
+from jax.experimental import pallas as pl
+from jax.experimental.pallas import tpu as pltpu
 from jax.sharding import PartitionSpec as P
+import functools
 
 epsilon = 1e-06
 
@@ -31,7 +34,7 @@
     return jnp.sum(running * onehot, axis=-1, dtype=jnp.int32)
 
 
-def per_device(
+def gathered_per_device(
     tokens,
     norm_gain,
     router,
@@ -100,6 +103,440 @@
     return total.astype(jnp.bfloat16)
 
 
+MESH = pl.DeviceIdType.MESH
+
+
+def fused_kernel(
+    n,
+    tokens_ref,
+    gain_ref,
+    router_ref,
+    ids_ref,
+    kind_ref,
+    wg_hbm,
+    wu_hbm,
+    wd_hbm,
+    sg_hbm,
+    su_hbm,
+    sd_hbm,
+    out_ref,
+    x_buf,
+    wt_buf,
+    wg,
+    wu,
+    wd,
+    sg,
+    su,
+    sd,
+    hid,
+    shid,
+    part,
+    sib_out,
+    sib_in,
+    rs_out,
+    rs_in,
+    dp_out,
+    dp_in,
+    w_sem,
+    ag_send,
+    ag_recv,
+    sx_send,
+    sx_recv,
+    wt_send,
+    wt_recv,
+    dp_send,
+    dp_recv,
+    sr_send,
+    sr_recv,
+    rs_send,
+    rs_recv,
+):
+    dp = lax.axis_index("dp")
+    me = lax.axis_index("expert")
+    core = lax.axis_index("tensor")
+    other = 1 - core
+    far = n // 2
+    rows, width = tokens_ref.shape
+    half = width // 2
+    cut = rows // 2
+    expert_count = router_ref.shape[1]
+    ring = (me % 2) * (n - 1 - me // 2) + (1 - me % 2) * (me // 2)
+
+    def at_ring(offset):
+        spot = (ring + offset + n) % n
+        late = spot // far
+        return late * (2 * (n - 1 - spot) + 1) + (1 - late) * (2 * spot)
+
+    def peer(offset):
+        return (dp, at_ring(offset), core)
+
+    sibling = (dp, me, other)
+    across = (1 - dp, me, core)
+
+    def left_slot(d):
+        return n - 1 if d == far else 2 * d - 1
+
+    def right_slot(d):
+        return n - 1 if d == far else 2 * d
+
+    def piece(k):
+        return pl.ds(k * cut, cut)
+
+    loads = [
+        pltpu.make_async_copy(wg_hbm.at[0], wg, w_sem.at[0]),
+        pltpu.make_async_copy(wu_hbm.at[0], wu, w_sem.at[1]),
+        pltpu.make_async_copy(wd_hbm.at[0, :, pl.ds(0, half)], wd.at[0], w_sem.at[2]),
+        pltpu.make_async_copy(wd_hbm.at[0, :, pl.ds(half, half)], wd.at[1], w_sem.at[3]),
+        pltpu.make_async_copy(sg_hbm, sg, w_sem.at[4]),
+        pltpu.make_async_copy(su_hbm, su, w_sem.at[5]),
+        pltpu.make_async_copy(sd_hbm.at[:, :, pl.ds(0, half)], sd.at[0], w_sem.at[6]),
+        pltpu.make_async_copy(sd_hbm.at[:, :, pl.ds(half, half)], sd.at[1], w_sem.at[7]),
+    ]
+    for load in loads:
+        load.start()
+
+    barrier = pltpu.get_barrier_semaphore()
+    greeted = [peer(d) for d in range(1, n)] + [sibling, across]
+    for device in greeted:
+        pl.semaphore_signal(barrier, inc=1, device_id=device, device_id_type=MESH)
+
+    values = tokens_ref[...].astype(jnp.float32)
+    inv_scale = lax.rsqrt(jnp.mean(values * values, axis=-1, keepdims=True) + epsilon)
+    normed = (values * inv_scale * gain_ref[...]).astype(jnp.bfloat16)
+    x_buf[0, 0] = normed[:, :half]
+    x_buf[0, 1] = normed[:, half:]
+    logits = jnp.dot(normed, router_ref[...], preferred_element_type=jnp.float32)
+    lanes = lax.broadcasted_iota(jnp.int32, (rows, expert_count), 1)
+    chosen = lanes < 0
+    for k in range(ids_ref.shape[1]):
+        chosen = chosen | (ids_ref[:, k : k + 1] == lanes)
+    scores = jnp.where(chosen, jax.nn.sigmoid(logits), 0.0)
+    weights = scores / jnp.sum(scores, axis=1, keepdims=True)
+    padded = jnp.concatenate(
+        [weights, jnp.zeros((rows, rows - expert_count), jnp.float32)], axis=1
+    )
+    wt_buf[0, 0:expert_count] = padded.T[0:expert_count]
+    flags = kind_ref[...].astype(jnp.float32)
+    wt_buf[0, expert_count : expert_count + 8] = jnp.broadcast_to(flags, (8, rows))
+
+    pl.semaphore_wait(barrier, len(greeted))
+
+    started = []
+
+    def remote(src, dst, send, recv, device):
+        return pltpu.make_async_remote_copy(
+            src_ref=src,
+            dst_ref=dst,
+            send_sem=send,
+            recv_sem=recv,
+            device_id=device,
+            device_id_type=MESH,
+        )
+
+    def send(*copy):
+        made = remote(*copy)
+        made.start()
+        started.append(made)
+
+    def gather_copy(way, d, k):
+        slot_of = (left_slot, right_slot)[way]
+        src = x_buf.at[0 if d == 1 else slot_of(d - 1), core, piece(k)]
+        dst = x_buf.at[slot_of(d), core, piece(k)]
+        return (
+            src,
+            dst,
+            ag_send.at[way, d - 1, k],
+            ag_recv.at[way, d - 1, k],
+            peer(1 if way == 0 else -1),
+        )
+
+    def swap_copy(way, d, k, mine):
+        slot = (left_slot, right_slot)[way](d)
+        block = x_buf.at[slot, core if mine else other, piece(k)]
+        return (block, block, sx_send.at[way, d - 1, k], sx_recv.at[way, d - 1, k], sibling)
+
+    def weight_copy(d):
+        slot = 2 * d - 1 if d < far else (n - 1 if d == far else 2 * (n - d))
+        return (wt_buf.at[0], wt_buf.at[slot], wt_send.at[slot], wt_recv.at[slot], peer(d))
+
+    for k in range(2):
+        for way in range(2):
+            send(*gather_copy(way, 1, k))
+        if k == 0:
+            send(wt_buf.at[0], wt_buf.at[n], wt_send.at[n], wt_recv.at[n], across)
+            send(x_buf.at[0, core], x_buf.at[n, core], dp_send.at[0], dp_recv.at[0], across)
+            for d in range(1, n):
+                send(*weight_copy(d))
+
+    def forward(d, k):
+        for way in range(2):
+            if d == far and way != k:
+                continue
+            remote(*gather_copy(way, d, k)).wait_recv()
+            if d + 1 < far or (d + 1 == far and way == k):
+                send(*gather_copy(way, d + 1, k))
+            send(*swap_copy(way, d, k, True))
+
+    def swapped(d):
+        for k in range(2):
+            for way in range(2):
+                if d == far and way != k:
+                    continue
+                remote(*swap_copy(way, d, k, False)).wait_recv()
+
+    def column(row):
+        return jnp.broadcast_to(row, (rows, rows)).T[:, 0:1]
+
+    def rows_of(slots, part_index):
+        blocks = [x_buf[slot, part_index] for slot in slots]
+        return blocks[0] if len(blocks) == 1 else jnp.concatenate(blocks, axis=0)
+
+    def double_dot(slots, low, high):
+        return jnp.dot(
+            rows_of(slots, 0), low, preferred_element_type=jnp.float32
+        ) + jnp.dot(rows_of(slots, 1), high, preferred_element_type=jnp.float32)
+
+    def expert_up_part(slots):
+        for slot in slots:
+            if slot != 0:
+                block = wt_buf.at[slot]
+                remote(
+                    block, block, wt_send.at[slot], wt_recv.at[slot], sibling
+                ).wait_recv()
+        gate_value = double_dot(slots, wg[0:half], wg[half:width])
+        up_value = double_dot(slots, wu[0:half], wu[half:width])
+        scale = [column(wt_buf[slot, pl.ds(me, 1), :]) for slot in slots]
+        scale = scale[0] if len(scale) == 1 else jnp.concatenate(scale, axis=0)
+        hidden = (gate_value / (1.0 + jnp.exp(-gate_value))) * up_value * scale
+        hid[0 : len(slots) * rows] = hidden.astype(jnp.bfloat16)
+
+    def give(slot):
+        return (
+            sib_out.at[slot],
+            sib_in.at[slot],
+            sr_send.at[slot],
+            sr_recv.at[slot],
+            sibling,
+        )
+
+    def expert_down_part(slots):
+        hidden = hid[0 : len(slots) * rows]
+        theirs = jnp.dot(hidden, wd[other], preferred_element_type=jnp.float32)
+        for i, slot in enumerate(slots):
+            block = theirs[i * rows : (i + 1) * rows]
+            if slot == 0:
+                part[n + 1] = block
+            else:
+                sib_out[slot] = block.astype(jnp.bfloat16)
+                send(*give(slot))
+        mine = jnp.dot(hidden, wd[core], preferred_element_type=jnp.float32)
+        for i, slot in enumerate(slots):
+            part[slot] = mine[i * rows : (i + 1) * rows]
+
+    def shared_part():
+        slots = (0, n)
+        flag = jnp.concatenate(
+            [column(wt_buf[slot, expert_count : expert_count + 1, :]) for slot in slots], axis=0
+        )
+        mine = theirs = None
+        for m, keep in enumerate((flag, 1.0 - flag)):
+            gate_value = double_dot(slots, sg[m, 0:half], sg[m, half:width])
+            up_value = double_dot(slots, su[m, 0:half], su[m, half:width])
+            hidden = (gate_value / (1.0 + jnp.exp(-gate_value))) * up_value * keep
+            shid[m] = hidden.astype(jnp.bfloat16)
+        def down(which):
+            return jnp.dot(
+                shid[0], sd[which, 0], preferred_element_type=jnp.float32
+            ) + jnp.dot(shid[1], sd[which, 1], preferred_element_type=jnp.float32)
+        theirs = down(other)
+        sib_out[0] = (theirs[:rows] + part[n + 1]).astype(jnp.bfloat16)
+        sib_out[n] = theirs[rows:].astype(jnp.bfloat16)
+        send(*give(n))
+        send(*give(0))
+        mine = down(core)
+        part[0] = part[0] + mine[:rows]
+        part[n] = mine[rows:]
+
+    def shared_return():
+        remote(*give(n)).wait_recv()
+        dp_out[...] = (part[n] + sib_in[n].astype(jnp.float32)).astype(jnp.bfloat16)
+        send(dp_out, dp_in, dp_send.at[1], dp_recv.at[1], across)
+
+    def reduce_copy(way, d, k):
+        return (
+            rs_out.at[way, d - 1, piece(k)],
+            rs_in.at[way, d - 1, piece(k)],
+            rs_send.at[way, d - 1, k],
+            rs_recv.at[way, d - 1, k],
+            peer(1 if way == 0 else -1),
+        )
+
+    def reduce_step(way, d, k):
+        slot = (right_slot, left_slot)[way](d)
+        total = part[slot, piece(k)] + sib_in[slot, piece(k)].astype(jnp.float32)
+        if d + 1 < far or (d + 1 == far and way == k):
+            remote(*reduce_copy(way, d + 1, k)).wait_recv()
+            total = total + rs_in[way, d, piece(k)].astype(jnp.float32)
+        rs_out[way, d - 1, piece(k)] = total.astype(jnp.bfloat16)
+        send(*reduce_copy(way, d, k))
+
+    for load in loads[:4]:
+        load.wait()
+    expert_up_part((0,))
+    forward(1, 0)
+    expert_down_part((0,))
+    for load in loads[4:]:
+        load.wait()
+    forward(1, 1)
+    swapped(1)
+    for d in range(1, far):
+        slots = (left_slot(d), right_slot(d))
+        expert_up_part(slots)
+        forward(d + 1, 0)
+        if d == 1:
+            remote(x_buf.at[0, core], x_buf.at[n, core], dp_send.at[0], dp_recv.at[0], across).wait_recv()
+            block = x_buf.at[n, core]
+            send(block, block, sx_send.at[0, far, 0], sx_recv.at[0, far, 0], sibling)
+        expert_down_part(slots)
+        forward(d + 1, 1)
+        if d == 1:
+            block = x_buf.at[n, other]
+            remote(block, block, sx_send.at[0, far, 0], sx_recv.at[0, far, 0], sibling).wait_recv()
+            block = wt_buf.at[n]
+            remote(block, block, wt_send.at[n], wt_recv.at[n], across).wait_recv()
+            shared_part()
+        swapped(d + 1)
+        if d == 2:
+            shared_return()
+    expert_up_part((n - 1,))
+    expert_down_part((n - 1,))
+    for slot in (left_slot(far - 1), right_slot(far - 1)):
+        remote(*give(slot)).wait_recv()
+    reduce_step(0, far - 1, 1)
+    reduce_step(1, far - 1, 0)
+    remote(*give(n - 1)).wait_recv()
+    reduce_step(0, far, 0)
+    reduce_step(1, far, 1)
+    for d in range(far - 2, 0, -1):
+        for slot in (left_slot(d), right_slot(d)):
+            remote(*give(slot)).wait_recv()
+    remote(*give(0)).wait_recv()
+    reduce_step(0, far - 1, 0)
+    reduce_step(1, far - 1, 1)
+    for d in range(far - 2, 0, -1):
+        reduce_step(0, d, 1)
+        reduce_step(1, d, 0)
+        reduce_step(0, d, 0)
+        reduce_step(1, d, 1)
+    remote(dp_out, dp_in, dp_send.at[1], dp_recv.at[1], across).wait_recv()
+    base = part[0] + sib_in[0].astype(jnp.float32) + dp_in[...].astype(jnp.float32)
+    part[0] = base
+    for k in (1, 0):
+        for way in (0, 1):
+            if far == 1 and way != k:
+                continue
+            remote(*reduce_copy(way, 1, k)).wait_recv()
+    for k in range(2):
+        total = part[0, piece(k)]
+        for way in range(2):
+            total = total + rs_in[way, 0, piece(k)].astype(jnp.float32)
+        out_ref[piece(k)] = total.astype(out_ref.dtype)
+    for made in started:
+        made.wait_send()
+
+
+def fused_per_device(
+    tokens,
+    norm_gain,
+    router,
+    expert_ids,
+    modality,
+    expert_gate,
+    expert_up,
+    expert_down,
+    shared_gate,
+    shared_up,
+    shared_down,
+):
+    n = lax.axis_size("expert")
+    rows, width = tokens.shape
+    half = width // 2
+    far = n // 2
+    hidden = expert_gate.shape[2]
+    shared = shared_gate.shape[2]
+    held = router.shape[1] + 8
+    bf16, f32 = jnp.bfloat16, jnp.float32
+    dma = pltpu.SemaphoreType.DMA
+    scratch = [
+        pltpu.VMEM((n + 1, 2, rows, half), bf16),
+        pltpu.VMEM((n + 1, held, rows), f32),
+        pltpu.VMEM((width, hidden), bf16),
+        pltpu.VMEM((width, hidden), bf16),
+        pltpu.VMEM((2, hidden, half), bf16),
+        pltpu.VMEM((2, width, shared), bf16),
+        pltpu.VMEM((2, width, shared), bf16),
+        pltpu.VMEM((2, 2, shared, half), bf16),
+        pltpu.VMEM((2 * rows, hidden), bf16),
+        pltpu.VMEM((2, 2 * rows, shared), bf16),
+        pltpu.VMEM((n + 2, rows, half), f32),
+        pltpu.VMEM((n + 1, rows, half), bf16),
+        pltpu.VMEM((n + 1, rows, half), bf16),
+        pltpu.VMEM((2, far, rows, half), bf16),
+        pltpu.VMEM((2, far, rows, half), bf16),
+        pltpu.VMEM((rows, half), bf16),
+        pltpu.VMEM((rows, half), bf16),
+        dma((8,)),
+        dma((2, far, 2)),
+        dma((2, far, 2)),
+        dma((2, far + 1, 2)),
+        dma((2, far + 1, 2)),
+        dma((n + 1,)),
+        dma((n + 1,)),
+        dma((2,)),
+        dma((2,)),
+        dma((n + 1,)),
+        dma((n + 1,)),
+        dma((2, far, 2)),
+        dma((2, far, 2)),
+    ]
+    vmem = pl.BlockSpec(memory_space=pltpu.VMEM)
+    anywhere = pl.BlockSpec(memory_space=pl.ANY)
+    return pl.pallas_call(
+        functools.partial(fused_kernel, n),
+        out_shape=jax.ShapeDtypeStruct((rows, half), bf16),
+        in_specs=[vmem] * 5 + [anywhere] * 6,
+        out_specs=vmem,
+        scratch_shapes=scratch,
+        compiler_params=pltpu.CompilerParams(
+            collective_id=0, has_side_effects=True, vmem_limit_bytes=60 * 1024 * 1024
+        ),
+    )(
+        tokens,
+        norm_gain.reshape(1, -1),
+        router,
+        expert_ids,
+        modality.reshape(1, -1),
+        expert_gate,
+        expert_up,
+        expert_down,
+        shared_gate,
+        shared_up,
+        shared_down,
+    )
+
+
+def per_device(*arrays):
+    tokens, expert_gate, router = arrays[0], arrays[5], arrays[2]
+    n = lax.axis_size("expert")
+    block_bytes = tokens.shape[0] * tokens.shape[1] * 2
+    weight_bytes = sum(2 * array.size for array in arrays[5:])
+    fits = 9 * n * block_bytes // 2 + weight_bytes < 40 * 1024 * 1024
+    square = tokens.shape[0] == 128 and lax.axis_size("tensor") == 2 and lax.axis_size("dp") == 2
+    if fits and square and n >= 6 and n % 2 == 0 and expert_gate.shape[0] == 1:
+        return fused_per_device(*arrays)
+    return gathered_per_device(*arrays)
+
+
 def solution(mesh):
     in_specs = (
         P(("dp", "expert"), None),

time: 200 us -> 80.8 us (0.40)
  waiting for transfers between devices: 108 us -> 0 us
  Pallas kernels: 0 us -> 60.6 us
  matrix products: 28.7 us -> 0 us
  between operations: 15.1 us -> 0.01 us
  starting transfers between devices: 12 us -> 0 us
  other arithmetic: 9.49 us -> 0 us
  blocking collectives: 4.22 us -> 0 us
    all_to_all x2 -> x0, waiting for transfers between devices: 108 us -> none  [the longest x1 58.8 us: per_device(): lax.all_to_all(outgoing, 'expert', split_axis=0, concat_axis=0, tiled=True)]
    pallas_call x0 -> x1, Pallas kernels: none -> 60.6 us  [fused_per_device(): pl.pallas_call(functools.partial(fused_kernel, n), out_shape=jax.ShapeDty...]
    dot_general x10 -> x0, matrix products: 28.7 us -> none  [the longest x1 5.71 us: per_device(): result = jnp.dot(hidden, expert_down[0], preferred_element_type=jnp.float32)]
    unnamed x19 -> x9, local copies, waits for them, and re-layouts: 2.15 us -> 19.8 us
    all_to_all x2 -> x0, starting transfers between devices: 11.7 us -> none  [the longest x1 7.31 us: per_device(): lax.all_to_all(outgoing, 'expert', split_axis=0, concat_axis=0, tiled=True)]
    gather x7 -> x0, local copies, waits for them, and re-layouts: 11.2 us -> none  [the longest x2 8.24 us: per_device(): picked = returned.reshape(-1, returned.shape[2])[target]]
    reshape x2 -> x0, local copies, waits for them, and re-layouts: 4.98 us -> none  [the longest x1 4.94 us: per_device(): down_blocks = shared_down.reshape(-1, pair_count, half_width)]
    reduce_sum x4 -> x0, other arithmetic: 4.33 us -> none  [the longest x1 2.97 us: per_device(): routed = jnp.sum(weights[:, :, None] * picked, axis=1)]
  transfers between devices with their start and end apart: 5 -> 0, of which waited for: 2 -> 0; matrix products, arithmetic and copies ran while one was open for 24% -> 0% of each run, Pallas kernels for 0% -> 0%
where the time goes in v1:
time: 80.8 us; the launch traced here: 80.4 us
  Pallas kernels  60.6 us (75%)
  local copies, waits for them, and re-layouts  19.8 us (25%)
    pallas_call x1, Pallas kernels, fused_per_device(): pl.pallas_call(functools.partial(fused_kernel, n), out_shape=jax.ShapeDty...  60.6 us
    unnamed x9, local copies, waits for them, and re-layouts  19.8 us

profile of v1, /device:TPU:0, one launch (start us, length us, event | category | flops | bytes accessed | tf_op | source)
XLA Modules:
  0.0 80.4 jit_solution(16729019943578093720)
XLA Ops:
  0.0 1.4 %copy.13.ids_ref = s32[128,4]{1,0:T(8,128)} copy(s32[128,4]{0,1:T(4,128)} %param.14) | data formatting | bytes 4096 | tf_op args[3]
  1.4 1.8 %copy.12.router_ref = bf16[2048,8]{1,0:T(8,128)(2,1)} copy(bf16[2048,8]{0,1:T(8,128)(2,1)} %param.13) | data formatting | bytes 65536 | tf_op args[2]
  3.2 0.0 copy-start
  3.2 3.8 %copy.16.sg_hbm = bf16[2,2048,176]{2,1,0:T(8,128)(2,1)} copy(bf16[2,2048,176]{1,2,0:T(8,128)(2,1)} %param.19) | data formatting | bytes 2883584 | tf_op args[8]
  7.0 3.7 %copy.17.su_hbm = bf16[2,2048,176]{2,1,0:T(8,128)(2,1)} copy(bf16[2,2048,176]{1,2,0:T(8,128)(2,1)} %param.20) | data formatting | bytes 2883584 | tf_op args[9]
  10.7 0.0 copy-done
  10.7 2.8 %copy.14.wg_hbm = bf16[1,2048,704]{2,1,0:T(8,128)(2,1)} copy(bf16[1,2048,704]{1,2,0:T(8,128)(2,1)S(1)} %copy-done) | data formatting | bytes 5767168 | tf_op args[5]
  13.5 4.6 %copy.15.wu_hbm = bf16[1,2048,704]{2,1,0:T(8,128)(2,1)} copy(bf16[1,2048,704]{1,2,0:T(8,128)(2,1)} %param.17) | data formatting | bytes 5767168 | tf_op args[6]
  18.1 60.6 %shard_map.109 = bf16[128,1024]{1,0:T(8,128)(2,1)} custom-call(bf16[128,2048]{1,0:T(8,128)(2,1)} %tokens_ref.1, f32[1,2048]{1,0:T(1,128)} %bitcast.2, bf16[2048,8]{1,0:T(8,128)(2,1)} %copy.12.router_ref, s32[128,4]{1,0:T(8,128)} %copy.13.ids_ref, s32[1,128]{1,0:T(1,128)} %bitcast.3, bf16[1,2048,704]{2,1,0:T(8,128)(2,1)} %copy.14.wg_hbm, ...), custom_call_target="tpu_custom_call" | custom-call | tf_op jit(solution)/shard_map/pallas_call | solution.py:504
  78.7 1.7 %copy.19 = bf16[128,1024]{1,0:T(8,128)(2,1)} copy(bf16[128,1024]{1,0:T(8,128)(2,1)} %shard_map.109) | data formatting | bytes 524288
Async XLA Ops:
  3.2 7.5 %copy-start = (bf16[1,2048,704]{1,2,0:T(8,128)(2,1)S(1)}, bf16[1,2048,704]{1,2,0:T(8,128)(2,1)}, u32[]{:S(2)}) copy-start(bf16[1,2048,704]{1,2,0:T(8,128)(2,1)} %param.16) | copy-start | bytes 8650756

commit v2 on v1

--- a/solution.py
+++ b/solution.py
@@ -101,6 +101,12 @@
     )
     total = shared_sum + routed
     return total.astype(jnp.bfloat16)
+
+
+def across_dot(left, right):
+    return lax.dot_general(
+        left, right, (((1,), (1,)), ((), ())), preferred_element_type=jnp.float32
+    )
 
 
 MESH = pl.DeviceIdType.MESH
@@ -159,7 +165,7 @@
     rows, width = tokens_ref.shape
     half = width // 2
     cut = rows // 2
-    expert_count = router_ref.shape[1]
+    expert_count = router_ref.shape[0]
     ring = (me % 2) * (n - 1 - me // 2) + (1 - me % 2) * (me // 2)
 
     def at_ring(offset):
@@ -205,17 +211,13 @@
     normed = (values * inv_scale * gain_ref[...]).astype(jnp.bfloat16)
     x_buf[0, 0] = normed[:, :half]
     x_buf[0, 1] = normed[:, half:]
-    logits = jnp.dot(normed, router_ref[...], preferred_element_type=jnp.float32)
-    lanes = lax.broadcasted_iota(jnp.int32, (rows, expert_count), 1)
-    chosen = lanes < 0
-    for k in range(ids_ref.shape[1]):
-        chosen = chosen | (ids_ref[:, k : k + 1] == lanes)
+    logits = across_dot(router_ref[...], normed)
+    named = lax.broadcasted_iota(jnp.int32, (expert_count, rows), 0)
+    chosen = named < 0
+    for k in range(ids_ref.shape[0]):
+        chosen = chosen | (ids_ref[k : k + 1, :] == named)
     scores = jnp.where(chosen, jax.nn.sigmoid(logits), 0.0)
-    weights = scores / jnp.sum(scores, axis=1, keepdims=True)
-    padded = jnp.concatenate(
-        [weights, jnp.zeros((rows, rows - expert_count), jnp.float32)], axis=1
-    )
-    wt_buf[0, 0:expert_count] = padded.T[0:expert_count]
+    wt_buf[0, 0:expert_count] = scores / jnp.sum(scores, axis=0, keepdims=True)
     flags = kind_ref[...].astype(jnp.float32)
     wt_buf[0, expert_count : expert_count + 8] = jnp.broadcast_to(flags, (8, rows))
 
@@ -259,89 +261,100 @@
         slot = 2 * d - 1 if d < far else (n - 1 if d == far else 2 * (n - d))
         return (wt_buf.at[0], wt_buf.at[slot], wt_send.at[slot], wt_recv.at[slot], peer(d))
 
-    for k in range(2):
+    for turn in range(2):
         for way in range(2):
-            send(*gather_copy(way, 1, k))
-        if k == 0:
+            send(*gather_copy(way, 1, (way + turn) % 2))
+        if turn == 0:
             send(wt_buf.at[0], wt_buf.at[n], wt_send.at[n], wt_recv.at[n], across)
             send(x_buf.at[0, core], x_buf.at[n, core], dp_send.at[0], dp_recv.at[0], across)
             for d in range(1, n):
                 send(*weight_copy(d))
 
-    def forward(d, k):
+    def forward(d, turn):
         for way in range(2):
-            if d == far and way != k:
-                continue
+            k = (way + turn) % 2
             remote(*gather_copy(way, d, k)).wait_recv()
-            if d + 1 < far or (d + 1 == far and way == k):
+            if d + 1 < far or (d + 1 == far and turn == 0):
                 send(*gather_copy(way, d + 1, k))
             send(*swap_copy(way, d, k, True))
 
-    def swapped(d):
-        for k in range(2):
-            for way in range(2):
-                if d == far and way != k:
-                    continue
-                remote(*swap_copy(way, d, k, False)).wait_recv()
+    def swapped(d, turn):
+        for way in range(2):
+            remote(*swap_copy(way, d, (way + turn) % 2, False)).wait_recv()
 
     def column(row):
         return jnp.broadcast_to(row, (rows, rows)).T[:, 0:1]
 
-    def rows_of(slots, part_index):
-        blocks = [x_buf[slot, part_index] for slot in slots]
+    def whole(*slots):
+        return [(slot, 0, rows) for slot in slots]
+
+    def joined(blocks):
         return blocks[0] if len(blocks) == 1 else jnp.concatenate(blocks, axis=0)
 
-    def double_dot(slots, low, high):
-        return jnp.dot(
-            rows_of(slots, 0), low, preferred_element_type=jnp.float32
-        ) + jnp.dot(rows_of(slots, 1), high, preferred_element_type=jnp.float32)
-
-    def expert_up_part(slots):
+    def rows_of(pieces, part_index):
+        return joined([x_buf[slot, part_index, lo : lo + size] for slot, lo, size in pieces])
+
+    def double_dot(pieces, low, high):
+        return across_dot(rows_of(pieces, 0), low) + across_dot(rows_of(pieces, 1), high)
+
+    def weights_here(*slots):
         for slot in slots:
-            if slot != 0:
-                block = wt_buf.at[slot]
-                remote(
-                    block, block, wt_send.at[slot], wt_recv.at[slot], sibling
-                ).wait_recv()
-        gate_value = double_dot(slots, wg[0:half], wg[half:width])
-        up_value = double_dot(slots, wu[0:half], wu[half:width])
-        scale = [column(wt_buf[slot, pl.ds(me, 1), :]) for slot in slots]
-        scale = scale[0] if len(scale) == 1 else jnp.concatenate(scale, axis=0)
+            block = wt_buf.at[slot]
+            remote(block, block, wt_send.at[slot], wt_recv.at[slot], sibling).wait_recv()
+
+    def expert_up_part(pieces):
+        count = sum(size for slot, lo, size in pieces)
+        gate_value = double_dot(pieces, wg[:, 0:half], wg[:, half:width])
+        up_value = double_dot(pieces, wu[:, 0:half], wu[:, half:width])
+        scale = joined(
+            [column(wt_buf[slot, pl.ds(me, 1), :])[lo : lo + size] for slot, lo, size in pieces]
+        )
         hidden = (gate_value / (1.0 + jnp.exp(-gate_value))) * up_value * scale
-        hid[0 : len(slots) * rows] = hidden.astype(jnp.bfloat16)
-
-    def give(slot):
+        hid[0:count] = hidden.astype(jnp.bfloat16)
+
+    def give(slot, lo=0, size=rows):
+        block = pl.ds(lo, size)
         return (
-            sib_out.at[slot],
-            sib_in.at[slot],
-            sr_send.at[slot],
-            sr_recv.at[slot],
+            sib_out.at[slot, block],
+            sib_in.at[slot, block],
+            sr_send.at[slot, lo // cut],
+            sr_recv.at[slot, lo // cut],
             sibling,
         )
 
-    def expert_down_part(slots):
-        hidden = hid[0 : len(slots) * rows]
+    def given(*pieces):
+        for piece_given in pieces:
+            remote(*give(*piece_given)).wait_recv()
+
+    def expert_down_part(pieces):
+        count = sum(size for slot, lo, size in pieces)
+        hidden = hid[0:count]
         theirs = jnp.dot(hidden, wd[other], preferred_element_type=jnp.float32)
-        for i, slot in enumerate(slots):
-            block = theirs[i * rows : (i + 1) * rows]
+        first = 0
+        for slot, lo, size in pieces:
+            block = theirs[first : first + size]
+            first += size
             if slot == 0:
                 part[n + 1] = block
             else:
-                sib_out[slot] = block.astype(jnp.bfloat16)
-                send(*give(slot))
+                sib_out[slot, lo : lo + size] = block.astype(jnp.bfloat16)
+                send(*give(slot, lo, size))
         mine = jnp.dot(hidden, wd[core], preferred_element_type=jnp.float32)
-        for i, slot in enumerate(slots):
-            part[slot] = mine[i * rows : (i + 1) * rows]
+        first = 0
+        for slot, lo, size in pieces:
+            part[slot, lo : lo + size] = mine[first : first + size]
+            first += size
 
     def shared_part():
         slots = (0, n)
+        pieces = whole(*slots)
         flag = jnp.concatenate(
             [column(wt_buf[slot, expert_count : expert_count + 1, :]) for slot in slots], axis=0
         )
         mine = theirs = None
         for m, keep in enumerate((flag, 1.0 - flag)):
-            gate_value = double_dot(slots, sg[m, 0:half], sg[m, half:width])
-            up_value = double_dot(slots, su[m, 0:half], su[m, half:width])
+            gate_value = double_dot(pieces, sg[m, :, 0:half], sg[m, :, half:width])
+            up_value = double_dot(pieces, su[m, :, 0:half], su[m, :, half:width])
             hidden = (gate_value / (1.0 + jnp.exp(-gate_value))) * up_value * keep
             shid[m] = hidden.astype(jnp.bfloat16)
         def down(which):
@@ -358,7 +371,7 @@
         part[n] = mine[rows:]
 
     def shared_return():
-        remote(*give(n)).wait_recv()
+        given((n,))
         dp_out[...] = (part[n] + sib_in[n].astype(jnp.float32)).astype(jnp.bfloat16)
         send(dp_out, dp_in, dp_send.at[1], dp_recv.at[1], across)
 
@@ -382,60 +395,72 @@
 
     for load in loads[:4]:
         load.wait()
-    expert_up_part((0,))
+    expert_up_part(whole(0))
     forward(1, 0)
-    expert_down_part((0,))
+    expert_down_part(whole(0))
     for load in loads[4:]:
         load.wait()
     forward(1, 1)
-    swapped(1)
-    for d in range(1, far):
-        slots = (left_slot(d), right_slot(d))
-        expert_up_part(slots)
+    for d in range(1, far - 1):
+        pieces = whole(left_slot(d), right_slot(d))
+        swapped(d, 0)
+        swapped(d, 1)
+        weights_here(left_slot(d), right_slot(d))
+        expert_up_part(pieces)
         forward(d + 1, 0)
         if d == 1:
-            remote(x_buf.at[0, core], x_buf.at[n, core], dp_send.at[0], dp_recv.at[0], across).wait_recv()
+            remote(
+                x_buf.at[0, core], x_buf.at[n, core], dp_send.at[0], dp_recv.at[0], across
+            ).wait_recv()
             block = x_buf.at[n, core]
             send(block, block, sx_send.at[0, far, 0], sx_recv.at[0, far, 0], sibling)
-        expert_down_part(slots)
+        expert_down_part(pieces)
         forward(d + 1, 1)
         if d == 1:
             block = x_buf.at[n, other]
             remote(block, block, sx_send.at[0, far, 0], sx_recv.at[0, far, 0], sibling).wait_recv()
-            block = wt_buf.at[n]
-            remote(block, block, wt_send.at[n], wt_recv.at[n], across).wait_recv()
+            weights_here(n)
             shared_part()
-        swapped(d + 1)
         if d == 2:
             shared_return()
-    expert_up_part((n - 1,))
-    expert_down_part((n - 1,))
-    for slot in (left_slot(far - 1), right_slot(far - 1)):
-        remote(*give(slot)).wait_recv()
-    reduce_step(0, far - 1, 1)
-    reduce_step(1, far - 1, 0)
-    remote(*give(n - 1)).wait_recv()
+    near = far - 1
+    early = [(right_slot(near), cut, cut), (left_slot(near), 0, cut)]
+    later = [(right_slot(near), 0, cut), (left_slot(near), cut, cut)]
+    last = whole(n - 1)
+    swapped(near, 0)
+    weights_here(left_slot(near), right_slot(near))
+    expert_up_part(early)
+    expert_down_part(early)
+    swapped(near, 1)
+    expert_up_part(later)
+    given(*early)
+    reduce_step(0, near, 1)
+    reduce_step(1, near, 0)
+    expert_down_part(later)
+    forward(far, 0)
+    weights_here(n - 1)
+    swapped(far, 0)
+    expert_up_part(last)
+    expert_down_part(last)
+    given(*last)
     reduce_step(0, far, 0)
     reduce_step(1, far, 1)
-    for d in range(far - 2, 0, -1):
-        for slot in (left_slot(d), right_slot(d)):
-            remote(*give(slot)).wait_recv()
-    remote(*give(0)).wait_recv()
-    reduce_step(0, far - 1, 0)
-    reduce_step(1, far - 1, 1)
+    given(*later)
+    for d in range(near - 1, 0, -1):
+        given(*whole(left_slot(d), right_slot(d)))
+    given(*whole(0))
+    remote(dp_out, dp_in, dp_send.at[1], dp_recv.at[1], across).wait_recv()
+    part[0] = part[0] + sib_in[0].astype(jnp.float32) + dp_in[...].astype(jnp.float32)
+    reduce_step(0, near, 0)
+    reduce_step(1, near, 1)
     for d in range(far - 2, 0, -1):
         reduce_step(0, d, 1)
         reduce_step(1, d, 0)
         reduce_step(0, d, 0)
         reduce_step(1, d, 1)
-    remote(dp_out, dp_in, dp_send.at[1], dp_recv.at[1], across).wait_recv()
-    base = part[0] + sib_in[0].astype(jnp.float32) + dp_in[...].astype(jnp.float32)
-    part[0] = base
-    for k in (1, 0):
-        for way in (0, 1):
-            if far == 1 and way != k:
-                continue
-            remote(*reduce_copy(way, 1, k)).wait_recv()
+    for turn in range(2):
+        for way in range(2):
+            remote(*reduce_copy(way, 1, (way + 1 + turn) % 2)).wait_recv()
     for k in range(2):
         total = part[0, piece(k)]
         for way in range(2):
@@ -470,11 +495,11 @@
     scratch = [
         pltpu.VMEM((n + 1, 2, rows, half), bf16),
         pltpu.VMEM((n + 1, held, rows), f32),
-        pltpu.VMEM((width, hidden), bf16),
-        pltpu.VMEM((width, hidden), bf16),
+        pltpu.VMEM((hidden, width), bf16),
+        pltpu.VMEM((hidden, width), bf16),
         pltpu.VMEM((2, hidden, half), bf16),
-        pltpu.VMEM((2, width, shared), bf16),
-        pltpu.VMEM((2, width, shared), bf16),
+        pltpu.VMEM((2, shared, width), bf16),
+        pltpu.VMEM((2, shared, width), bf16),
         pltpu.VMEM((2, 2, shared, half), bf16),
         pltpu.VMEM((2 * rows, hidden), bf16),
         pltpu.VMEM((2, 2 * rows, shared), bf16),
@@ -494,8 +519,8 @@
         dma((n + 1,)),
         dma((2,)),
         dma((2,)),
-        dma((n + 1,)),
-        dma((n + 1,)),
+        dma((n + 1, 2)),
+        dma((n + 1, 2)),
         dma((2, far, 2)),
         dma((2, far, 2)),
     ]
@@ -513,14 +538,14 @@
     )(
         tokens,
         norm_gain.reshape(1, -1),
-        router,
-        expert_ids,
+        router.T,
+        expert_ids.T,
         modality.reshape(1, -1),
-        expert_gate,
-        expert_up,
+        jnp.swapaxes(expert_gate, 1, 2),
+        jnp.swapaxes(expert_up, 1, 2),
         expert_down,
-        shared_gate,
-        shared_up,
+        jnp.swapaxes(shared_gate, 1, 2),
+        jnp.swapaxes(shared_up, 1, 2),
         shared_down,
     )
 

time: 80.8 us -> 62.3 us (0.77)
  local copies, waits for them, and re-layouts: 19.8 us -> 1.67 us
    unnamed x9 -> x1, local copies, waits for them, and re-layouts: 19.8 us -> 1.67 us
where the time goes in v2:
time: 62.3 us; the launch traced here: 62.2 us
  Pallas kernels  60.5 us (97%)
  local copies, waits for them, and re-layouts  1.67 us (3%)
    pallas_call x1, Pallas kernels, fused_per_device(): pl.pallas_call(functools.partial(fused_kernel, n), out_shape=jax.ShapeDty...  60.5 us
    unnamed x1, local copies, waits for them, and re-layouts  1.67 us

profile of v2, /device:TPU:0, one launch (start us, length us, event | category | flops | bytes accessed | tf_op | source)
XLA Modules:
  0.0 62.2 jit_solution(11025764070886630662)
XLA Ops:
  0.0 60.5 %shard_map.109 = bf16[128,1024]{1,0:T(8,128)(2,1)} custom-call(bf16[128,2048]{1,0:T(8,128)(2,1)} %tokens_ref.1, f32[1,2048]{1,0:T(1,128)} %bitcast.13, bf16[8,2048]{1,0:T(8,128)(2,1)} %bitcast.12, s32[4,128]{1,0:T(4,128)} %bitcast.14, s32[1,128]{1,0:T(1,128)} %bitcast.15, bf16[1,704,2048]{2,1,0:T(8,128)(2,1)} %bitcast.8, bf16[1,704,2048]{2,1,0:T(8,128)(2,1)} %bitcast.9, ...), custom_call_target="tpu_custom_call" | custom-call | tf_op jit(solution)/shard_map/pallas_call | solution.py:529
  60.5 1.7 %copy.13 = bf16[128,1024]{1,0:T(8,128)(2,1)} copy(bf16[128,1024]{1,0:T(8,128)(2,1)} %shard_map.109) | data formatting | bytes 524288
